TPU v7x, 256 devices: a whole 4x4x8 slice. The times are simulated.
256 devices in a mesh: cuts: 32 (over z, x), mode: 8 (over y, core).
Axes of the slice: x: 4, y: 4, z: 8, core: 2. Of those that a mesh axis runs over, the one named last changes fastest.
Arguments:
- sliced_state: bfloat16 [8, 64, 4, 128, 2, 128], P(None, 'cuts', None, 'mode'), may hold values from -0.75 to 0.75
- gate_blocks: bfloat16 [32, 2, 128, 128], P('cuts'), may hold values from -0.375 to 0.375
- gate_slot: int32 [32], replicated, may hold values from 0 to 31, each once
- samples: int32 [8, 4096], replicated, may hold values from 0 to 65535
Outputs:
- amplitudes: float32 [32, 128, 2, 128], P('cuts', 'mode')
- sample_probs: float32 [8, 4096], replicated
- xeb_score: float32 [8], replicated
Inputs may be any that keep to these rules, and one draw needn't show every extreme that they name: `gate_slot`: a permutation: every gate block has its own row of gate_blocks. `samples`: flat index s * 128 * 128 + p * 128 + q.
All inputs are finite; a program needn't handle non-finite values.
Results may differ from a plain program's by a relative error of at most 0.022.
Values may be sent and summed in bfloat16 or wider, within the bound.
A program may use at most 64 MiB of HBM per device.

v0:
```python
import functools

import jax
import jax.numpy as jnp
from jax import lax
from jax.sharding import Mesh
from jax.sharding import PartitionSpec as P

MODE = ("mode_0", "mode_1")
CUTS = ("cuts_0", "cuts_1")
CUTS_MODE = ("cuts_0", "cuts_1", "mode_0", "mode_1")


def gathered_by_axis(array, axes, dim):
    if not axes:
        return array
    nearer = lax.all_gather(array, axes[-1], axis=dim, tiled=True)
    return gathered_by_axis(nearer, axes[:-1], dim)


def cut_along(array, dim, count):
    before, after = (array.shape[:dim], array.shape[dim + 1 :])
    return jnp.moveaxis(array.reshape(*before, count, -1, *after), dim, 0)


def sum_at_owner(array, axis, dim):
    tiles = cut_along(array, dim, lax.axis_size(axis))
    arrived = lax.all_to_all(tiles, axis, split_axis=0, concat_axis=0, tiled=True)
    return arrived.astype(jnp.float32).sum(axis=0)


def by_axis(array, axes):
    return functools.reduce(lax.psum, axes, array)


def apply_gates(tensor, blocks):
    real_part = blocks[:, 0]
    imag_part = blocks[:, 1]
    stacked = jnp.concatenate(
        [
            jnp.concatenate([real_part, imag_part], axis=2),
            jnp.concatenate([-imag_part, real_part], axis=2),
        ],
        axis=1,
    )
    layout = tensor.shape
    flattened = tensor.reshape(layout[0], -1, 2 * layout[-1])
    product = jnp.einsum("crk,ckn->crn", flattened, stacked, preferred_element_type=jnp.float32)
    return product.astype(jnp.bfloat16).reshape(layout)


def select_rows(table, wanted):
    count = table.shape[0]
    onehot = (wanted[:, None] == jnp.arange(count, dtype=jnp.int32)[None, :]).astype(table.dtype)
    picked = jnp.dot(onehot, table.reshape(count, -1), preferred_element_type=jnp.float32)
    return picked.astype(table.dtype).reshape((wanted.shape[0],) + table.shape[1:])


def on_device(sliced_state, gate_blocks, gate_slot, samples):
    circuits = sliced_state.shape[0]
    spectator = sliced_state.shape[2]
    width = sliced_state.shape[5]
    layer_count = gate_slot.shape[0] // (2 * circuits)
    circuit_ids = jnp.arange(circuits, dtype=jnp.int32)
    tensor = lax.all_to_all(sliced_state, MODE, split_axis=0, concat_axis=3, tiled=True)
    local_count = tensor.shape[0]
    local_ids = lax.axis_index(MODE) * local_count + jnp.arange(local_count, dtype=jnp.int32)
    gathered = gathered_by_axis(gate_blocks, CUTS, 0)

    def fetch_gates(layer_index, gate_kind):
        return select_rows(
            gathered, gate_slot[(local_ids * layer_count + layer_index) * 2 + gate_kind]
        )

    for layer_index in range(layer_count):
        tensor = apply_gates(tensor, fetch_gates(layer_index, 0))
        tensor = jnp.swapaxes(tensor, 3, 5)
        tensor = apply_gates(tensor, fetch_gates(layer_index, 1))
        tensor = jnp.swapaxes(tensor, 3, 5)
    summed = jnp.sum(tensor.astype(jnp.float32), axis=1)
    summed = lax.all_to_all(
        summed.astype(jnp.bfloat16), MODE, split_axis=2, concat_axis=0, tiled=True
    ).astype(summed.dtype)
    local_rows = summed.shape[2]
    summed = summed.reshape(circuits * spectator, local_rows, 2, width)
    amplitudes = sum_at_owner(summed.astype(jnp.bfloat16), CUTS, 0)
    row_count = amplitudes.shape[0]
    first_row = lax.axis_index(CUTS) * row_count
    first_col = lax.axis_index(MODE) * local_rows
    magnitude = amplitudes[:, :, 0, :] ** 2 + amplitudes[:, :, 1, :] ** 2
    row_sums = jnp.sum(magnitude, axis=(1, 2))
    owner_circuit = (first_row + jnp.arange(row_count, dtype=jnp.int32)) // spectator
    norm_part = jnp.sum(
        jnp.where(owner_circuit[None, :] == circuit_ids[:, None], row_sums[None, :], 0.0), axis=1
    )
    plane_size = width * width
    spec_index = samples // plane_size
    row_index = samples // width % width
    col_index = samples % width
    local_row = circuit_ids[:, None] * spectator + spec_index - first_row
    local_col = row_index - first_col
    is_owned = (
        (local_row >= 0) & (local_row < row_count) & (local_col >= 0) & (local_col < local_rows)
    )
    cell_index = jnp.where(is_owned, local_row * local_rows + local_col, -1)
    cell_count = row_count * local_rows
    cell_onehot = (
        cell_index[:, :, None] == jnp.arange(cell_count, dtype=jnp.int32)[None, None, :]
    ).astype(jnp.float32)
    picked_rows = jnp.einsum("csr,rw->csw", cell_onehot, magnitude.reshape(cell_count, width))
    col_match = col_index[:, :, None] == jnp.arange(width, dtype=jnp.int32)[None, None, :]
    sample_mass = jnp.sum(jnp.where(col_match, picked_rows, 0.0), axis=2)
    dimension_scale = float(spectator * plane_size)
    mass_total, norm_total = (by_axis(sample_mass, CUTS_MODE), by_axis(norm_part, CUTS_MODE))
    sample_probs = mass_total * dimension_scale / norm_total[:, None]
    xeb_score = jnp.mean(sample_probs, axis=1)
    return (amplitudes, sample_probs, xeb_score)


def solution(mesh):
    split = Mesh(mesh.devices.reshape(8, 4, 4, 2), ("cuts_0", "cuts_1", "mode_0", "mode_1"))
    placed = (P(None, CUTS, None, MODE, None, None), P(CUTS, None, None, None), P(), P())
    return jax.shard_map(
        on_device,
        mesh=split,
        in_specs=placed,
        out_specs=(P(CUTS, MODE, None, None), P(), P()),
        check_vma=False,
    )
```

profile of v0, /device:TPU:1, one launch (start us, length us, event | category | flops | bytes accessed | tf_op | source)
XLA Modules:
  0.0 329.6 jit_solution(11438945458227351211)
XLA Ops:
  7.2 12.4 %all_gather.6 = bf16[4,2,128,128]{3,2,1,0:T(8,128)(2,1)} all-gather(bf16[1,2,128,128]{3,2,1,0:T(8,128)(2,1)} %param.5), channel_id=1, replica_groups=mesh['cuts_0'=8,'cuts_1'=4,'mode_0'=4,'mode_1'=2] {'cuts_1'}, dimensions={0}, use_global_device_ids=true | all-gather | bytes 327680 | tf_op jit(solution)/shard_map/all_gather | solution.py:17
  19.6 7.8 %all-to-all-start = ((bf16[8,2,4,16,2,128]{5,4,3,2,1,0:T(2,128)(2,1)}), bf16[8,2,4,16,2,128]{5,4,3,2,1,0:T(2,128)(2,1)S(1)}, u32[]{:S(2)}, u32[]{:S(2)}) async-start(bf16[8,2,4,16,2,128]{5,4,3,2,1,0:T(2,128)(2,1)} %param.4), calls=%async_computation | async-start | bytes 1048576 | tf_op jit(solution)/shard_map/all_to_all | solution.py:65
  27.4 1.5 fusion.82
  28.9 7.9 %all-to-all-done = bf16[8,2,4,16,2,128]{5,4,3,2,1,0:T(2,128)(2,1)S(1)} async-done(((bf16[8,2,4,16,2,128]{5,4,3,2,1,0:T(2,128)(2,1)}), bf16[8,2,4,16,2,128]{5,4,3,2,1,0:T(2,128)(2,1)S(1)}, u32[]{:S(2)}, u32[]{:S(2)}) %all-to-all-start) | async-done | bytes 524320 | tf_op jit(solution)/shard_map/all_to_all | solution.py:65
  37.2 23.6 %all-gather.2.cloned.1.call-done = bf16[32,2,128,128]{3,2,1,0:T(8,128)(2,1)} async-done(((bf16[4,2,128,128]{3,2,1,0:T(8,128)(2,1)}), bf16[32,2,128,128]{3,2,1,0:T(8,128)(2,1)}) %all-gather.2.cloned.1.call-update) | async-done | bytes 2097168 | tf_op jit(solution)/shard_map/all_gather | solution.py:17
  60.8 3.6 %fusion.6 = f32[1,32768]{1,0:T(1,128)S(1)} fusion(bf16[4,8,256,128]{3,2,1,0:T(8,128)(2,1)} %bitcast.126, s32[]{:T(128)} %bitcast.2), kind=kOutput, calls=%fused_computation.8 | convolution fusion | flops 2097184 | bytes 2228228 | tf_op jit(solution)/shard_map/dot_general | solution.py:55
  64.4 1.9 fusion.4
  66.3 1.9 fusion.2
  68.3 1.8 fusion
  70.9 0.5 copy.13
  71.8 0.6 copy.14
  72.9 0.6 copy.15
  74.0 1.2 reduce_sum.58
  75.2 1.0 copy.16
  76.2 9.2 %all-to-all-start.1 = ((bf16[1,4,128,2,128]{4,3,1,0,2:T(2,128)(2,1)}), bf16[1,4,128,2,128]{4,3,1,0,2:T(2,128)(2,1)S(1)}, u32[]{:S(2)}, u32[]{:S(2)}) async-start(bf16[1,4,128,2,128]{4,3,1,0,2:T(2,128)(2,1)} %copy.16), calls=%async_computation.1 | async-start | bytes 524288 | tf_op jit(solution)/shard_map/all_to_all | solution.py:81
  85.3 6.5 %all-to-all-done.1 = bf16[1,4,128,2,128]{4,3,1,0,2:T(2,128)(2,1)S(1)} async-done(((bf16[1,4,128,2,128]{4,3,1,0,2:T(2,128)(2,1)}), bf16[1,4,128,2,128]{4,3,1,0,2:T(2,128)(2,1)S(1)}, u32[]{:S(2)}, u32[]{:S(2)}) %all-to-all-start.1) | async-done | bytes 262176 | tf_op jit(solution)/shard_map/all_to_all | solution.py:81
  91.9 0.7 copy.18
  92.6 6.8 %all-to-all-start.2 = ((bf16[32,1,16,2,128]{4,2,3,1,0:T(8,128)(2,1)}), bf16[32,1,16,2,128]{4,2,3,1,0:T(8,128)(2,1)S(1)}, u32[]{:S(2)}, u32[]{:S(2)}) async-start(bf16[32,1,16,2,128]{4,2,3,1,0:T(8,128)(2,1)} %bitcast.48), calls=%async_computation.2 | async-start | bytes 524288 | tf_op jit(solution)/shard_map/all_to_all | solution.py:28
  99.9 10.1 %all-to-all-done.2 = bf16[32,1,16,2,128]{4,2,3,1,0:T(8,128)(2,1)S(1)} async-done(((bf16[32,1,16,2,128]{4,2,3,1,0:T(8,128)(2,1)}), bf16[32,1,16,2,128]{4,2,3,1,0:T(8,128)(2,1)S(1)}, u32[]{:S(2)}, u32[]{:S(2)}) %all-to-all-start.2) | async-done | bytes 262176 | tf_op jit(solution)/shard_map/all_to_all | solution.py:28
  110.1 3.6 %select_reduce_fusion = f32[8,4096]{1,0:T(8,128)} fusion(s32[8,4096]{1,0:T(8,128)S(1)} %get-tuple-element.53, s32[8,4096]{1,0:T(8,128)S(1)} %get-tuple-element.52, f32[1,16,2,128]{3,1,2,0:T(8,128)S(1)} %bitcast.149), kind=kOutput, calls=%fused_computation | convolution fusion | flops 147298304 | bytes 409600 | tf_op jit(solution)/shard_map/csr,rw->csw/dot_general | solution.py:110
  113.7 63.6 %all-reduce.5.cloned.1.call-done = f32[8,4096]{1,0:T(8,128)} async-done(((f32[8,4096]{1,0:T(8,128)}), f32[8,4096]{1,0:T(8,128)}) %all-reduce.5.cloned.1.call-update) | async-done | bytes 131088 | tf_op jit(solution)/shard_map/psum | solution.py:33
  177.4 50.2 %all-reduce.7.cloned.1.call-done = f32[8,4096]{1,0:T(8,128)} async-done(((f32[8,4096]{1,0:T(8,128)}), f32[8,4096]{1,0:T(8,128)}) %all-reduce.7.cloned.1.call-update) | async-done | bytes 131088 | tf_op jit(solution)/shard_map/psum | solution.py:33
  227.8 49.1 %all-reduce.9.cloned.1.call-done = f32[8,4096]{1,0:T(8,128)} async-done(((f32[8,4096]{1,0:T(8,128)}), f32[8,4096]{1,0:T(8,128)}) %all-reduce.9.cloned.1.call-update) | async-done | bytes 131088 | tf_op jit(solution)/shard_map/psum | solution.py:33
  276.9 0.6 fusion.63
  277.5 0.6 compare_select_fusion
  278.2 13.7 %psum.60 = f32[8]{0:T(128)S(1)} all-reduce(f32[8]{0:T(128)S(1)} %compare_select_fusion), channel_id=1, replica_groups=mesh['cuts_0'=8,'cuts_1'=4,'mode_0'=4,'mode_1'=2] {'cuts_0'}, use_global_device_ids=true, to_apply=%region_8.9 | all-reduce | flops 8 | bytes 64 | tf_op jit(solution)/shard_map/psum | solution.py:33
  291.9 8.4 %psum.61 = f32[8]{0:T(128)S(1)} all-reduce(f32[8]{0:T(128)S(1)} %psum.60), channel_id=1, replica_groups=mesh['cuts_0'=8,'cuts_1'=4,'mode_0'=4,'mode_1'=2] {'cuts_1'}, use_global_device_ids=true, to_apply=%region_9.10 | all-reduce | flops 8 | bytes 64 | tf_op jit(solution)/shard_map/psum | solution.py:33
  300.3 7.4 %psum.62 = f32[8]{0:T(128)S(1)} all-reduce(f32[8]{0:T(128)S(1)} %psum.61), channel_id=1, replica_groups=mesh['cuts_0'=8,'cuts_1'=4,'mode_0'=4,'mode_1'=2] {'mode_0'}, use_global_device_ids=true, to_apply=%region_10.11 | all-reduce | flops 8 | bytes 64 | tf_op jit(solution)/shard_map/psum | solution.py:33
  307.6 12.5 %psum.63 = f32[8]{0:T(128)S(1)} all-reduce(f32[8]{0:T(128)S(1)} %psum.62), channel_id=1, replica_groups=mesh['cuts_0'=8,'cuts_1'=4,'mode_0'=4,'mode_1'=2] {'mode_1'}, use_global_device_ids=true, to_apply=%region_11.12 | all-reduce | flops 8 | bytes 64 | tf_op jit(solution)/shard_map/psum | solution.py:33
  320.2 0.6 copy.19
  320.8 1.8 fusion.81
  322.5 0.5 broadcast_multiply_fusion
  (40 shorter events, 3.3 us)
Async XLA Ops:
  7.2 53.6 %all-gather.2.cloned.1.call-start = ((), (), s32[]{:S(2)}) async-start(), calls=%async_computation.3 | async-start | bytes 2359296 | tf_op jit(solution)/shard_map/all_gather | solution.py:17
  19.6 17.1 %all-to-all-start = ((bf16[8,2,4,16,2,128]{5,4,3,2,1,0:T(2,128)(2,1)}), bf16[8,2,4,16,2,128]{5,4,3,2,1,0:T(2,128)(2,1)S(1)}, u32[]{:S(2)}, u32[]{:S(2)}) async-start(bf16[8,2,4,16,2,128]{5,4,3,2,1,0:T(2,128)(2,1)} %param.4), calls=%async_computation | async-start | bytes 1048576 | tf_op jit(solution)/shard_map/all_to_all | solution.py:65
  60.8 3.6 %copy-start = (bf16[32,2,128,128]{3,2,1,0:T(8,128)(2,1)S(1)}, bf16[32,2,128,128]{3,2,1,0:T(8,128)(2,1)}, u32[]{:S(2)}) copy-start(bf16[32,2,128,128]{3,2,1,0:T(8,128)(2,1)} %all-gather.2.cloned.1.call-done) | copy-start | bytes 6291460
  73.8 25.8 %copy-start.1 = (s32[8,4096]{1,0:T(8,128)S(1)}, s32[8,4096]{1,0:T(8,128)}, u32[]{:S(2)}) copy-start(s32[8,4096]{1,0:T(8,128)} %param.7) | copy-start | bytes 393220
  76.2 15.6 %all-to-all-start.1 = ((bf16[1,4,128,2,128]{4,3,1,0,2:T(2,128)(2,1)}), bf16[1,4,128,2,128]{4,3,1,0,2:T(2,128)(2,1)S(1)}, u32[]{:S(2)}, u32[]{:S(2)}) async-start(bf16[1,4,128,2,128]{4,3,1,0,2:T(2,128)(2,1)} %copy.16), calls=%async_computation.1 | async-start | bytes 524288 | tf_op jit(solution)/shard_map/all_to_all | solution.py:81
  92.6 17.5 %all-to-all-start.2 = ((bf16[32,1,16,2,128]{4,2,3,1,0:T(8,128)(2,1)}), bf16[32,1,16,2,128]{4,2,3,1,0:T(8,128)(2,1)S(1)}, u32[]{:S(2)}, u32[]{:S(2)}) async-start(bf16[32,1,16,2,128]{4,2,3,1,0:T(8,128)(2,1)} %bitcast.48), calls=%async_computation.2 | async-start | bytes 524288 | tf_op jit(solution)/shard_map/all_to_all | solution.py:28
  99.4 78.0 %all-reduce.5.cloned.1.call-start = ((), (), s32[]{:S(2)}) async-start(), calls=%async_computation.4 | async-start | bytes 262144 | tf_op jit(solution)/shard_map/psum | solution.py:33
  113.7 114.0 %all-reduce.7.cloned.1.call-start = ((), (), s32[]{:S(2)}) async-start(), calls=%async_computation.5 | async-start | bytes 262144 | tf_op jit(solution)/shard_map/psum | solution.py:33
  177.4 99.5 %all-reduce.9.cloned.1.call-start = ((), (), s32[]{:S(2)}) async-start(), calls=%async_computation.6 | async-start | bytes 262144 | tf_op jit(solution)/shard_map/psum | solution.py:33
  227.7 93.1 %all-reduce.11.cloned.1.call-start = ((), (), s32[]{:S(2)}) async-start(), calls=%async_computation.7 | async-start | bytes 262144 | tf_op jit(solution)/shard_map/psum | solution.py:33
Sparse Core Ops, SparseCore 0:
  19.8 40.9 all-gather.1
  113.8 63.5 all-reduce.4
  179.7 47.9 all-reduce.6
  229.8 47.0 all-reduce.8
  279.3 31.9 all-reduce.10
where the time goes:
time: 330 us
  waiting for transfers between devices  211 us (64%)
  blocking collectives  54.4 us (16%)
  starting transfers between devices  24.1 us (7%)
  matrix products  14 us (4%)
  between operations  14 us (4%)
  local copies, waits for them, and re-layouts  6.8 us (2%)
  other arithmetic  5.13 us (2%)
    psum x4, waiting for transfers between devices, by_axis(): return functools.reduce(lax.psum, axes, array)  163 us
    psum x4, blocking collectives, by_axis(): return functools.reduce(lax.psum, axes, array)  42 us
    all_gather x1, waiting for transfers between devices, gathered_by_axis(): nearer = lax.all_gather(array, axes[-1], axis=dim, tiled=True)  23.6 us
    all_gather x1, blocking collectives, gathered_by_axis(): nearer = lax.all_gather(array, axes[-1], axis=dim, tiled=True)  12.4 us
    all_to_all x1, waiting for transfers between devices, sum_at_owner(): lax.all_to_all(tiles, axis, split_axis=0, concat_axis=0, tiled=True)  10.1 us
    dot_general x4, matrix products, select_rows(): jnp.dot(onehot, table.reshape(count, -1), preferred_element_type=jnp.floa...  9.17 us
    all_to_all x1, starting transfers between devices, on_device(): lax.all_to_all(summed.astype(jnp.bfloat16), MODE, split_axis=2, concat_ax...  9.15 us
    all_to_all x1, waiting for transfers between devices, on_device(): lax.all_to_all(sliced_state, MODE, split_axis=0, concat_axis=3, tiled=True)  7.88 us
  transfers between devices with their start and end apart: 8, of which 7 were waited for; matrix products, arithmetic and copies ran while one was open for 1% of the time, Pallas kernels for 0%

commit v1 on v0

v1 whole, which is shorter than its diff:
```python
import jax
import jax.numpy as jnp
from jax import lax
from jax.experimental import pallas as pl
from jax.experimental.pallas import tpu as pltpu
from jax.sharding import Mesh
from jax.sharding import PartitionSpec as P

AXES = ("z", "x", "y", "core")
NZ, NX, NY, NC = 8, 4, 4, 2
ROWS = NZ * NX
PLANE = NX * NY * NC
G = 128
PP = G // (NY * NC)
MESH = pl.DeviceIdType.MESH
F32, BF16 = jnp.float32, jnp.bfloat16


def mm(a, b):
    return jnp.dot(a, b, preferred_element_type=F32)


def kernel(
    slot_ref, state_hbm, gates_hbm, samples_hbm, amp_ref, probs_ref, xeb_ref,
    state_v, gate_v, samp_v, part, rs, gr, sel, xs, msg, agg, agx, fin, prow, zbuf, tile,
    load_sem, send_sem, recv_sem,
):
    z, x, y, core = (lax.axis_index(name) for name in AXES)
    zx = z * NX + x
    pj = x * (NY * NC) + y * NC + core

    def zx_peer(k):
        return (lax.rem(z + k // NX, NZ), lax.rem(x + lax.rem(k, NX), NX), y, core)

    def plane_peer(k):
        dx, m = k // (NY * NC), lax.rem(k, NY * NC)
        return (z, lax.rem(x + dx, NX), lax.rem(y + m // NC, NY), lax.rem(core + lax.rem(m, NC), NC))

    def remote(src, dst, i, peer):
        return pltpu.make_async_remote_copy(
            src_ref=src, dst_ref=dst, send_sem=send_sem.at[i], recv_sem=recv_sem.at[i],
            device_id=peer, device_id_type=MESH,
        )

    def wait_bytes(ref, sem):
        pltpu.make_async_copy(ref, ref, sem).wait()

    chunk = pl.ds(pl.multiple_of(pj * G, G), G)
    load_gate = pltpu.make_async_copy(gates_hbm, gate_v, load_sem.at[0])
    load_state = pltpu.make_async_copy(state_hbm, state_v, load_sem.at[1])
    load_samp = pltpu.make_async_copy(samples_hbm.at[:, chunk], samp_v, load_sem.at[2])
    load_gate.start()
    load_state.start()
    load_samp.start()

    barrier = pltpu.get_barrier_semaphore()

    def greet(k, carry):
        pl.semaphore_signal(barrier, inc=1, device_id=zx_peer(k), device_id_type=MESH)
        pl.semaphore_signal(barrier, inc=1, device_id=plane_peer(k), device_id_type=MESH)
        return carry

    lax.fori_loop(1, 32, greet, 0)
    load_gate.wait()
    load_state.wait()
    for c in range(NZ):
        for s in range(NX):
            part[c * NX + s] = (state_v[c, 0, s].astype(F32) + state_v[c, 1, s].astype(F32)).astype(BF16)
    pl.semaphore_wait(barrier, 62)

    own_gate = pltpu.make_async_copy(gate_v.at[pj], gr.at[zx], recv_sem.at[0])
    own_gate.start()

    def send_gate(k, carry):
        peer = zx_peer(k)
        remote(gate_v.at[peer[1] * (NY * NC) + y * NC + core], gr.at[zx], 0, peer).start()
        return carry

    lax.fori_loop(1, ROWS, send_gate, 0)
    own_part = pltpu.make_async_copy(part.at[zx], rs.at[zx], recv_sem.at[1])
    own_part.start()

    def send_part(k, carry):
        peer = zx_peer(k)
        remote(part.at[peer[0] * NX + peer[1]], rs.at[zx], 1, peer).start()
        return carry

    lax.fori_loop(1, ROWS, send_part, 0)

    wait_bytes(gr, recv_sem.at[0])
    for g in range(4):
        sel[g] = gr[slot_ref[z * 4 + g]]
    own_sel = pltpu.make_async_copy(sel, agg.at[pj], recv_sem.at[2])
    own_sel.start()

    def send_sel(k, carry):
        remote(sel, agg.at[pj], 2, plane_peer(k)).start()
        return carry

    lax.fori_loop(1, PLANE, send_sel, 0)

    wait_bytes(rs, recv_sem.at[1])
    total = rs[0].astype(F32)
    for i in range(1, ROWS):
        total = total + rs[i].astype(F32)
    xs[...] = total
    msg[0:PP] = xs[pl.ds(0, PP, stride=2), :].astype(BF16)
    msg[PP : 2 * PP] = xs[pl.ds(1, PP, stride=2), :].astype(BF16)
    own_msg = pltpu.make_async_copy(msg, agx.at[pj], recv_sem.at[3])
    own_msg.start()

    def send_msg(k, carry):
        remote(msg, agx.at[pj], 3, plane_peer(k)).start()
        return carry

    lax.fori_loop(1, PLANE, send_msg, 0)

    wait_bytes(agg, recv_sem.at[2])

    def gate(g):
        both = agg[:, g].astype(F32).reshape(2 * G, G)
        return both[:G].astype(BF16), both[G:].astype(BF16)

    def product(first, second):
        (ar, ai), (br, bi) = first, second
        four = mm(jnp.concatenate([ar, ai], axis=0), jnp.concatenate([br, bi], axis=1))
        return four[:G, :G] - four[G:, G:], four[:G, G:] + four[G:, :G]

    qr, qi = product(gate(0), gate(2))
    pr, pi = product(gate(1), gate(3))
    q_mat = jnp.concatenate(
        [jnp.concatenate([qr, qi], axis=1), jnp.concatenate([-qi, qr], axis=1)], axis=0
    ).astype(BF16)
    prt, pit = pr.T, pi.T
    p_mat = jnp.concatenate(
        [jnp.concatenate([prt, -pit], axis=1), jnp.concatenate([pit, prt], axis=1)], axis=0
    ).astype(BF16)

    wait_bytes(agx, recv_sem.at[3])
    flat = jnp.concatenate(
        [agx[:, 0:PP].reshape(NX * G, G), agx[:, PP : 2 * PP].reshape(NX * G, G)], axis=1
    )
    turned = mm(flat, q_mat).astype(BF16)

    load_samp.wait()
    wanted = samp_v[pl.ds(z, 1), :]
    column = jnp.broadcast_to(wanted & (G - 1), (G, G))
    line = jnp.broadcast_to(wanted >> 7, (G, G))
    lines = lax.broadcasted_iota(jnp.int32, (G, G), 0)
    picked = jnp.zeros((G, G), F32)
    norms = jnp.zeros((G, G), F32)
    for s in range(NX):
        block = turned[s * G : (s + 1) * G]
        out = mm(p_mat, jnp.concatenate([block[:, :G], block[:, G:]], axis=0))
        fin[s] = out
        mag = out[:G] * out[:G] + out[G:] * out[G:]
        norms = norms + mag
        found = jnp.take_along_axis(mag, column, axis=1)
        picked = jnp.where(line == lines + s * G, found, picked)
    norm = jnp.sum(norms, axis=(0, 1), keepdims=True)
    mass = jnp.sum(picked, axis=0, keepdims=True)
    prow[0] = mass * float(NX * G * G) / norm

    own_row = pltpu.make_async_copy(prow.at[0], zbuf.at[z], recv_sem.at[4])
    own_row.start()

    def send_row(k, carry):
        remote(prow.at[0], zbuf.at[z], 4, (lax.rem(z + k, NZ), x, y, core)).start()
        return carry

    lax.fori_loop(1, NZ, send_row, 0)
    first = pl.multiple_of((y * NC + core) * PP, PP)
    amp_ref[pl.ds(0, PP, stride=2), :] = fin[x, pl.ds(first, PP), :]
    amp_ref[pl.ds(1, PP, stride=2), :] = fin[x, pl.ds(G + first, PP), :]
    wait_bytes(zbuf, recv_sem.at[4])
    for c in range(NZ):
        tile[pl.ds(c, 1), :] = zbuf[c]

    own_tile = pltpu.make_async_copy(tile, probs_ref.at[:, chunk], recv_sem.at[5])
    own_tile.start()

    def send_tile(k, carry):
        remote(tile, probs_ref.at[:, chunk], 5, plane_peer(k)).start()
        return carry

    lax.fori_loop(1, PLANE, send_tile, 0)
    wait_bytes(gr.at[pl.ds(0, ROWS - 1)], send_sem.at[0])
    wait_bytes(rs.at[pl.ds(0, ROWS - 1)], send_sem.at[1])
    wait_bytes(agg.at[pl.ds(0, PLANE - 1)], send_sem.at[2])
    wait_bytes(agx.at[pl.ds(0, PLANE - 1)], send_sem.at[3])
    wait_bytes(zbuf.at[pl.ds(0, NZ - 1)], send_sem.at[4])
    wait_bytes(probs_ref, recv_sem.at[5])
    wait_bytes(probs_ref.at[:, pl.ds(0, G * (PLANE - 1))], send_sem.at[5])
    means = jnp.sum(probs_ref[...], axis=1, keepdims=True) * (1.0 / (PLANE * G))
    spot = lax.broadcasted_iota(jnp.int32, (NZ, G), 0) == lax.broadcasted_iota(jnp.int32, (NZ, G), 1)
    xeb_ref[...] = jnp.sum(jnp.where(spot, means, 0.0), axis=0, keepdims=True)


def on_device(sliced_state, gate_blocks, gate_slot, samples):
    state = sliced_state.reshape(NZ, 2, NX, 2 * PP, G)
    gates = gate_blocks.reshape(PLANE, 8, G)
    vmem, hbm = pl.BlockSpec(memory_space=pltpu.VMEM), pl.BlockSpec(memory_space=pl.ANY)
    amp, probs, xeb = pl.pallas_call(
        kernel,
        out_shape=(
            jax.ShapeDtypeStruct((2 * PP, G), F32),
            jax.ShapeDtypeStruct((NZ, PLANE * G), F32),
            jax.ShapeDtypeStruct((1, G), F32),
        ),
        in_specs=[pl.BlockSpec(memory_space=pltpu.SMEM), hbm, hbm, hbm],
        out_specs=(vmem, vmem, vmem),
        scratch_shapes=[
            pltpu.VMEM((NZ, 2, NX, 2 * PP, G), BF16),
            pltpu.VMEM((PLANE, 8, G), BF16),
            pltpu.VMEM((NZ, G), jnp.int32),
            pltpu.VMEM((ROWS, 2 * PP, G), BF16),
            pltpu.VMEM((ROWS, 2 * PP, G), BF16),
            pltpu.VMEM((ROWS, 8, G), BF16),
            pltpu.VMEM((4, 8, G), BF16),
            pltpu.VMEM((2 * PP, G), F32),
            pltpu.VMEM((2 * PP, G), BF16),
            pltpu.VMEM((PLANE, 4, 8, G), BF16),
            pltpu.VMEM((PLANE, 2 * PP, G), BF16),
            pltpu.VMEM((NX, 2 * G, G), F32),
            pltpu.VMEM((1, 1, G), F32),
            pltpu.VMEM((NZ, 1, G), F32),
            pltpu.VMEM((NZ, G), F32),
            pltpu.SemaphoreType.DMA((3,)),
            pltpu.SemaphoreType.DMA((6,)),
            pltpu.SemaphoreType.DMA((6,)),
        ],
        compiler_params=pltpu.CompilerParams(collective_id=0, has_side_effects=True),
        name="amplitudes",
    )(gate_slot, state, gates, samples)
    return amp.reshape(1, PP, 2, G), probs, xeb[0, :NZ]


def solution(mesh):
    split = Mesh(mesh.devices.reshape(NZ, NX, NY, NC), AXES)
    cuts, mode = ("z", "x"), ("y", "core")
    return jax.shard_map(
        on_device,
        mesh=split,
        in_specs=(P(None, cuts, None, mode, None, None), P(cuts, None, None, None), P(), P()),
        out_specs=(P(cuts, mode, None, None), P(), P()),
        check_vma=False,
    )
```

time: 330 us -> 46 us (0.14)
  waiting for transfers between devices: 211 us -> 0 us
  blocking collectives: 54.4 us -> 0 us
  Pallas kernels: 0 us -> 41.1 us
  starting transfers between devices: 24.1 us -> 0 us
  matrix products: 14 us -> 0 us
  between operations: 14 us -> 0.65 us
  other arithmetic: 5.13 us -> 0 us
    psum x4 -> x0, waiting for transfers between devices: 163 us -> none  [by_axis(): return functools.reduce(lax.psum, axes, array)]
    psum x4 -> x0, blocking collectives: 42 us -> none  [by_axis(): return functools.reduce(lax.psum, axes, array)]
    pallas_call x0 -> x1, Pallas kernels: none -> 41.1 us  [on_device(): pl.pallas_call(kernel, out_shape=(jax.ShapeDtypeStruct((2 * PP, G), F32),...]
    all_to_all x3 -> x0, waiting for transfers between devices: 24.5 us -> none  [the longest x1 10.1 us: sum_at_owner(): lax.all_to_all(tiles, axis, split_axis=0, concat_axis=0, tiled=True)]
    all_to_all x3 -> x0, starting transfers between devices: 23.7 us -> none  [the longest x1 9.15 us: on_device(): lax.all_to_all(summed.astype(jnp.bfloat16), MODE, split_axis=2, concat_ax...]
    all_gather x1 -> x0, waiting for transfers between devices: 23.6 us -> none  [gathered_by_axis(): nearer = lax.all_gather(array, axes[-1], axis=dim, tiled=True)]
    dot_general x9 -> x0, matrix products: 14 us -> none  [the longest x4 9.17 us: select_rows(): jnp.dot(onehot, table.reshape(count, -1), preferred_element_type=jnp.floa...]
    all_gather x1 -> x0, blocking collectives: 12.4 us -> none  [gathered_by_axis(): nearer = lax.all_gather(array, axes[-1], axis=dim, tiled=True)]
  transfers between devices with their start and end apart: 8 -> 0, of which waited for: 7 -> 0; matrix products, arithmetic and copies ran while one was open for 1% -> 0% of each run, Pallas kernels for 0% -> 0%
where the time goes in v1:
time: 46 us; the launch traced here: 45.8 us
  Pallas kernels  41.1 us (89%)
  local copies, waits for them, and re-layouts  4.02 us (9%)
  between operations  0.65 us (1%)
    pallas_call x1, Pallas kernels, on_device(): pl.pallas_call(kernel, out_shape=(jax.ShapeDtypeStruct((2 * PP, G), F32),...  41.1 us
    unnamed x4, local copies, waits for them, and re-layouts  3.51 us

profile of v1, /device:TPU:1, one launch (start us, length us, event | category | flops | bytes accessed | tf_op | source)
XLA Modules:
  0.0 45.8 jit_solution(17549931085210161876)
XLA Ops:
  0.6 41.1 %amplitudes.1 = (f32[32,128]{1,0:T(8,128)}, f32[8,4096]{1,0:T(8,128)}, f32[1,128]{1,0:T(1,128)}) custom-call(s32[32]{0:T(128)} %slot_ref.1, bf16[8,2,4,32,128]{4,3,2,1,0:T(8,128)(2,1)} %bitcast.5, bf16[32,8,128]{2,1,0:T(8,128)(2,1)} %bitcast.6, s32[8,4096]{1,0:T(8,128)} %samples_hbm.1), custom_call_target="tpu_custom_call" | custom-call | tf_op jit(solution)/shard_map/amplitudes/pallas_call | solution.py:203
  41.7 0.0 copy-start
  41.8 0.6 %copy-done = f32[1,128]{1,0:T(1,128)S(1)} copy-done((f32[1,128]{1,0:T(1,128)S(1)}, f32[1,128]{1,0:T(1,128)}, u32[]{:S(2)}) %copy-start) | copy-done | bytes 536
  42.4 0.5 %slice_bitcast_fusion = f32[8]{0:T(128)} fusion(f32[1,128]{1,0:T(1,128)S(1)} %copy-done), kind=kLoop, calls=%fused_computation | loop fusion | bytes 64 | tf_op jit(solution)/shard_map/squeeze | solution.py:235
  42.9 1.3 %copy.9 = f32[1,16,2,128]{3,2,1,0:T(2,128)} copy(f32[1,16,2,128]{3,2,1,0:T(2,128)} %bitcast.7) | data formatting | bytes 32768
  44.2 1.6 %copy.10 = f32[8,4096]{1,0:T(8,128)} copy(f32[8,4096]{1,0:T(8,128)} %get-tuple-element.13) | data formatting | bytes 262144
Async XLA Ops:
  41.7 0.6 %copy-start = (f32[1,128]{1,0:T(1,128)S(1)}, f32[1,128]{1,0:T(1,128)}, u32[]{:S(2)}) copy-start(f32[1,128]{1,0:T(1,128)} %get-tuple-element.8) | copy-start | bytes 1540

commit v2 on v0

v2 whole, which is shorter than its diff:
```python
import jax
import jax.numpy as jnp
from jax import lax
from jax.experimental import pallas as pl
from jax.experimental.pallas import tpu as pltpu
from jax.sharding import Mesh
from jax.sharding import PartitionSpec as P

AXES = ("z", "x", "y", "core")
NZ, NX, NY, NC = 8, 4, 4, 2
ROWS = NZ * NX
CHIPS = NX * NY
PLANE = CHIPS * NC
G = 128
PP = G // (NY * NC)
CHUNKS = 4096 // G // NC
MESH = pl.DeviceIdType.MESH
F32, BF16 = jnp.float32, jnp.bfloat16


def hops(offset):
    return sum(min(d, n - d) for d, n in zip(offset, (NZ, NX, NY, NC)))


def far_first(offsets):
    return sorted((o for o in offsets if any(o)), key=hops, reverse=True)


OVER_CUTS = far_first([(dz, dx, 0, 0) for dz in range(NZ) for dx in range(NX)])
IN_PLANE = far_first([(0, dx, dy, dc) for dx in range(NX) for dy in range(NY) for dc in range(NC)])
SAME_CORE = [o for o in IN_PLANE if o[3] == 0]
OVER_X = far_first([(0, dx, 0, 0) for dx in range(NX)])
OVER_Z = far_first([(dz, 0, 0, 0) for dz in range(NZ)])
GREETED = far_first(set(OVER_CUTS) | set(IN_PLANE))
PARTNER = (0, 0, 0, 1)
GATE, SEL, SWAP, SUMS, LINES, PROBS, HALF, FIRST = range(8)


def mm(a, b):
    return jnp.dot(a, b, preferred_element_type=F32)


def scope(name):
    return jax.named_scope(name)


def exchange(
    slot_hbm, state_hbm, gates_hbm, samples_hbm, amp_ref, probs_ref,
    slot_s, state_v, gate_v, samp_v, asked, part, xr, zs, zr, gr, sel, agg, xs, msg, agx, fin, mags, prow, zbuf,
    load_sem, send_sem, recv_sem,
):
    at = [lax.axis_index(name) for name in AXES]
    turn = [[i] + [lax.rem(i + d, n) for d in range(1, n)] for i, n in zip(at, (NZ, NX, NY, NC))]
    z, x, y, core = at
    zx, chip = z * NX + x, x * NY + y

    def peer(offset):
        return tuple(turn[axis][d] for axis, d in enumerate(offset))

    def send(src, dst, i, offset, j=None):
        pltpu.make_async_remote_copy(
            src_ref=src, dst_ref=dst, send_sem=send_sem.at[i], recv_sem=recv_sem.at[i if j is None else j],
            device_id=peer(offset), device_id_type=MESH,
        ).start()

    def keep(src, dst, i):
        pltpu.make_async_copy(src, dst, recv_sem.at[i]).start()

    def wait_bytes(ref, sem):
        pltpu.make_async_copy(ref, ref, sem).wait()

    with scope("greet"):
        load_state = pltpu.make_async_copy(state_hbm, state_v, load_sem.at[0])
        load_gate = pltpu.make_async_copy(gates_hbm, gate_v, load_sem.at[1])
        load_slot = pltpu.make_async_copy(slot_hbm, slot_s, load_sem.at[2])
        half = pl.ds(pl.multiple_of(core * CHUNKS * G, G), CHUNKS * G)
        load_samp = pltpu.make_async_copy(samples_hbm.at[:, half], samp_v, load_sem.at[3])
        for load in (load_state, load_gate, load_slot, load_samp):
            load.start()
        barrier = pltpu.get_barrier_semaphore()
        for offset in GREETED:
            pl.semaphore_signal(barrier, inc=1, device_id=peer(offset), device_id_type=MESH)
    with scope("sum"):
        load_state.wait()
        for c in range(NZ):
            for s in range(NX):
                part[c, s] = (state_v[c, 0, s].astype(F32) + state_v[c, 1, s].astype(F32)).astype(BF16)
        load_gate.wait()
    with scope("barrier"):
        pl.semaphore_wait(barrier, len(GREETED))

    with scope("send_a"):
        for offset in OVER_CUTS:
            _, px, _, _ = peer(offset)
            send(gate_v.at[core * CHIPS + px * NY + y], gr.at[zx], GATE, offset)
        order = [dz for dz, *_ in OVER_Z] + [0]
        for i, dz in enumerate(order):
            for offset in OVER_X:
                dx = offset[1]
                send(part.at[turn[0][dz], turn[1][dx]], xr.at[i, dx - 1], FIRST, offset, FIRST + i)
        keep(gate_v.at[core * CHIPS + chip], gr.at[zx], GATE)
    own = None
    for i, dz in enumerate(order):
        with scope("sums_%d" % i):
            wait_bytes(xr.at[i], recv_sem.at[FIRST + i])
            own = part[turn[0][dz], x].astype(F32)
            for dx in range(1, NX):
                own = own + xr[i, dx - 1].astype(F32)
            if dz:
                zs[i] = own.astype(BF16)
                send(zs.at[i], zr.at[dz - 1], SUMS, OVER_Z[i])

    with scope("wait_gate"):
        load_slot.wait()
        wait_bytes(gr, recv_sem.at[GATE])
    with scope("send_sel"):
        for g in range(4):
            sel[g] = gr[slot_s[z * 4 + g]]
        for offset in SAME_CORE:
            send(sel, agg.at[core, chip], SEL, offset)
        keep(sel, agg.at[core, chip], SEL)
    with scope("wait_sums"):
        wait_bytes(zr, recv_sem.at[SUMS])
    with scope("send_lines"):
        for i in range(NZ - 1):
            own = own + zr[i].astype(F32)
        xs[...] = own
        msg[0:PP] = xs[pl.ds(0, PP, stride=2), :].astype(BF16)
        msg[PP : 2 * PP] = xs[pl.ds(1, PP, stride=2), :].astype(BF16)
        place = chip * NC + core
        for offset in IN_PLANE:
            send(msg, agx.at[place], LINES, offset)
        keep(msg, agx.at[place], LINES)
    with scope("wait_sel"):
        wait_bytes(agg.at[0], recv_sem.at[SEL])
    with scope("swap"):
        send(agg.at[core], agg.at[core], SWAP, PARTNER)
        wait_bytes(agg.at[0], recv_sem.at[SWAP])

    def gate(g):
        both = agg[:, :, g].astype(F32).reshape(2 * G, G)
        return both[:G].astype(BF16), both[G:].astype(BF16)

    def product(first, second):
        (ar, ai), (br, bi) = first, second
        four = mm(jnp.concatenate([ar, ai], axis=0), jnp.concatenate([br, bi], axis=1))
        return four[:G, :G] - four[G:, G:], four[:G, G:] + four[G:, :G]

    with scope("mats"):
        qr, qi = product(gate(0), gate(2))
        pr, pi = product(gate(1), gate(3))
        q_mat = jnp.concatenate(
            [jnp.concatenate([qr, qi], axis=1), jnp.concatenate([-qi, qr], axis=1)], axis=0
        ).astype(BF16)
        prt, pit = pr.T, pi.T
        p_mat = jnp.concatenate(
            [jnp.concatenate([prt, -pit], axis=1), jnp.concatenate([pit, prt], axis=1)], axis=0
        ).astype(BF16)
    with scope("wait_lines"):
        load_samp.wait()
        for k in range(CHUNKS):
            asked[k] = samp_v[:, k * G : (k + 1) * G]
        wait_bytes(agx, recv_sem.at[LINES])
    with scope("math"):
        flat = jnp.concatenate(
            [agx[:, 0:PP].reshape(NX * G, G), agx[:, PP : 2 * PP].reshape(NX * G, G)], axis=1
        )
        turned = mm(flat, q_mat).astype(BF16)
        norms = jnp.zeros((G, G), F32)
        for s in range(NX):
            block = turned[s * G : (s + 1) * G]
            out = mm(p_mat, jnp.concatenate([block[:, :G], block[:, G:]], axis=0))
            fin[s] = out
            mag = out[:G] * out[:G] + out[G:] * out[G:]
            mags[s * G : (s + 1) * G] = mag
            norms = norms + mag
        scale = float(NX * G * G) / jnp.sum(norms, axis=(0, 1), keepdims=True)
    with scope("look_up"):
        lines = lax.broadcasted_iota(jnp.int32, (8, G), 0)
        for k in range(CHUNKS):
            wanted = asked[k, pl.ds(z, 1), :]
            column = jnp.broadcast_to(wanted & (G - 1), (8, G))
            line = jnp.broadcast_to(wanted >> 7, (8, G)) - lines
            picked = jnp.zeros((8, G), F32)
            for r in range(0, NX * G, 8):
                found = jnp.take_along_axis(mags[r : r + 8], column, axis=1)
                picked = jnp.where(line == r, found, picked)
            prow[k : k + 1] = jnp.sum(picked, axis=0, keepdims=True) * scale

    with scope("send_c"):
        for offset in OVER_Z:
            send(prow, zbuf.at[z], PROBS, offset)
        keep(prow, zbuf.at[z], PROBS)
        first = pl.multiple_of((y * NC + core) * PP, PP)
        amp_ref[pl.ds(0, PP, stride=2), :] = fin[x, pl.ds(first, PP), :]
        amp_ref[pl.ds(1, PP, stride=2), :] = fin[x, pl.ds(G + first, PP), :]
        wait_bytes(gr.at[pl.ds(0, ROWS - 1)], send_sem.at[GATE])
        wait_bytes(xr, send_sem.at[FIRST])
        wait_bytes(zr, send_sem.at[SUMS])
        wait_bytes(agg.at[0, pl.ds(0, CHIPS - 1)], send_sem.at[SEL])
        wait_bytes(agg.at[0], send_sem.at[SWAP])
        wait_bytes(agx.at[pl.ds(0, PLANE - 1)], send_sem.at[LINES])
        wait_bytes(zbuf.at[pl.ds(0, NZ - 1)], send_sem.at[PROBS])
    with scope("wait_c"):
        wait_bytes(zbuf, recv_sem.at[PROBS])
    with scope("send_d"):
        for c in range(NZ):
            probs_ref[core, c] = zbuf[c]
        send(probs_ref.at[core], probs_ref.at[core], HALF, PARTNER)
    with scope("wait_d"):
        wait_bytes(probs_ref.at[0], recv_sem.at[HALF])
        wait_bytes(probs_ref.at[0], send_sem.at[HALF])


def hand_out(amp_v, probs_v, amp_hbm, probs_hbm, xeb_ref, lined, sem):
    keep_amp = pltpu.make_async_copy(amp_v, amp_hbm, sem.at[0])
    keep_amp.start()
    total = jnp.zeros((NZ, G), F32)
    for half in range(NC):
        for k in range(CHUNKS):
            run = jnp.concatenate([probs_v[half, c, k : k + 1] for c in range(NZ)], axis=0)
            lined[:, (half * CHUNKS + k) * G : (half * CHUNKS + k + 1) * G] = run
            total = total + run
    keep_probs = pltpu.make_async_copy(lined, probs_hbm, sem.at[1])
    keep_probs.start()
    means = jnp.sum(total, axis=1, keepdims=True) * (1.0 / (NC * CHUNKS * G))
    spot = lax.broadcasted_iota(jnp.int32, (NZ, G), 0) == lax.broadcasted_iota(jnp.int32, (NZ, G), 1)
    xeb_ref[...] = jnp.sum(jnp.where(spot, means, 0.0), axis=0, keepdims=True)[:, :NZ]
    keep_amp.wait()
    keep_probs.wait()


def on_device(sliced_state, gate_blocks, gate_slot, samples):
    state = sliced_state.reshape(NZ, 2, NX, 2 * PP, G)
    gates = gate_blocks.reshape(PLANE, 8, G)
    hbm, vmem = pl.BlockSpec(memory_space=pl.ANY), pl.BlockSpec(memory_space=pltpu.VMEM)
    block = (2 * PP, G)
    amp, probs = pl.pallas_call(
        exchange,
        out_shape=(pltpu.VMEM(block, F32), pltpu.VMEM((NC, NZ, CHUNKS, G), F32)),
        in_specs=[hbm] * 4,
        out_specs=(vmem, vmem),
        scratch_shapes=[
            pltpu.SMEM((ROWS,), jnp.int32),
            pltpu.VMEM((NZ, 2, NX) + block, BF16),
            pltpu.VMEM((PLANE, 8, G), BF16),
            pltpu.VMEM((NZ, CHUNKS * G), jnp.int32),
            pltpu.VMEM((CHUNKS, NZ, G), jnp.int32),
            pltpu.VMEM((NZ, NX) + block, BF16),
            pltpu.VMEM((NZ, NX - 1) + block, BF16),
            pltpu.VMEM((NZ - 1,) + block, BF16),
            pltpu.VMEM((NZ - 1,) + block, BF16),
            pltpu.VMEM((ROWS, 8, G), BF16),
            pltpu.VMEM((4, 8, G), BF16),
            pltpu.VMEM((NC, CHIPS, 4, 8, G), BF16),
            pltpu.VMEM(block, F32),
            pltpu.VMEM(block, BF16),
            pltpu.VMEM((PLANE,) + block, BF16),
            pltpu.VMEM((NX, 2 * G, G), F32),
            pltpu.VMEM((NX * G, G), F32),
            pltpu.VMEM((CHUNKS, G), F32),
            pltpu.VMEM((NZ, CHUNKS, G), F32),
            pltpu.SemaphoreType.DMA((4,)),
            pltpu.SemaphoreType.DMA((FIRST + NZ,)),
            pltpu.SemaphoreType.DMA((FIRST + NZ,)),
        ],
        compiler_params=pltpu.CompilerParams(collective_id=0, has_side_effects=True),
        name="amplitudes",
    )(gate_slot, state, gates, samples)
    amp, probs, xeb = pl.pallas_call(
        hand_out,
        out_shape=(
            jax.ShapeDtypeStruct(block, F32),
            jax.ShapeDtypeStruct((NZ, NC * CHUNKS * G), F32),
            jax.ShapeDtypeStruct((1, NZ), F32),
        ),
        in_specs=[vmem, vmem],
        out_specs=(hbm, hbm, vmem),
        scratch_shapes=[pltpu.VMEM((NZ, NC * CHUNKS * G), F32), pltpu.SemaphoreType.DMA((2,))],
        name="hand_out",
    )(*(pltpu.with_memory_space_constraint(array, pltpu.VMEM) for array in (amp, probs)))
    return amp.reshape(1, PP, 2, G), probs, xeb.reshape(NZ)


def solution(mesh):
    split = Mesh(mesh.devices.reshape(NZ, NX, NY, NC), AXES)
    cuts, mode = ("z", "x"), ("y", "core")
    return jax.shard_map(
        on_device,
        mesh=split,
        in_specs=(P(None, cuts, None, mode, None, None), P(cuts, None, None, None), P(), P()),
        out_specs=(P(cuts, mode, None, None), P(), P()),
        check_vma=False,
    )
```

time: 330 us -> 36.4 us (0.11)
  waiting for transfers between devices: 211 us -> 0 us
  blocking collectives: 54.4 us -> 0 us
  Pallas kernels: 0 us -> 35.6 us
  starting transfers between devices: 24.1 us -> 0 us
  matrix products: 14 us -> 0 us
  between operations: 14 us -> 0.64 us
  local copies, waits for them, and re-layouts: 6.8 us -> 0 us
  other arithmetic: 5.13 us -> 0 us
    psum x4 -> x0, waiting for transfers between devices: 163 us -> none  [by_axis(): return functools.reduce(lax.psum, axes, array)]
    psum x4 -> x0, blocking collectives: 42 us -> none  [by_axis(): return functools.reduce(lax.psum, axes, array)]
    pallas_call x0 -> x2, Pallas kernels: none -> 35.6 us  [the longest x1 34.4 us: on_device(): pl.pallas_call(exchange, out_shape=(pltpu.VMEM(block, F32), pltpu.VMEM((N...]
    all_to_all x3 -> x0, waiting for transfers between devices: 24.5 us -> none  [the longest x1 10.1 us: sum_at_owner(): lax.all_to_all(tiles, axis, split_axis=0, concat_axis=0, tiled=True)]
    all_to_all x3 -> x0, starting transfers between devices: 23.7 us -> none  [the longest x1 9.15 us: on_device(): lax.all_to_all(summed.astype(jnp.bfloat16), MODE, split_axis=2, concat_ax...]
    all_gather x1 -> x0, waiting for transfers between devices: 23.6 us -> none  [gathered_by_axis(): nearer = lax.all_gather(array, axes[-1], axis=dim, tiled=True)]
    dot_general x9 -> x0, matrix products: 14 us -> none  [the longest x4 9.17 us: select_rows(): jnp.dot(onehot, table.reshape(count, -1), preferred_element_type=jnp.floa...]
    all_gather x1 -> x0, blocking collectives: 12.4 us -> none  [gathered_by_axis(): nearer = lax.all_gather(array, axes[-1], axis=dim, tiled=True)]
  transfers between devices with their start and end apart: 8 -> 0, of which waited for: 7 -> 0; matrix products, arithmetic and copies ran while one was open for 1% -> 0% of each run, Pallas kernels for 0% -> 0%
where the time goes in v2:
time: 36.4 us; the launch traced here: 36.3 us
  Pallas kernels  35.6 us (98%)
  between operations  0.64 us (2%)
    pallas_call x1, Pallas kernels, on_device(): pl.pallas_call(exchange, out_shape=(pltpu.VMEM(block, F32), pltpu.VMEM((N...  34.4 us
    pallas_call x1, Pallas kernels, on_device(): pl.pallas_call(hand_out, out_shape=(jax.ShapeDtypeStruct(block, F32), jax...  1.26 us

profile of v2, /device:TPU:1, one launch (start us, length us, event | category | flops | bytes accessed | tf_op | source)
XLA Modules:
  0.0 36.3 jit_solution(9250273796034615016)
XLA Ops:
  0.6 34.4 %amplitudes.1 = (f32[32,128]{1,0:T(8,128)S(1)}, f32[2,8,16,128]{3,2,1,0:T(8,128)S(1)}) custom-call(s32[32]{0:T(128)} %slot_hbm.1, bf16[8,2,4,32,128]{4,3,2,1,0:T(8,128)(2,1)} %bitcast.4, bf16[32,8,128]{2,1,0:T(8,128)(2,1)} %bitcast.5, s32[8,4096]{1,0:T(8,128)} %samples_hbm.1), custom_call_target="tpu_custom_call" | custom-call | tf_op jit(solution)/shard_map/amplitudes/pallas_call | solution.py:238
  35.0 1.3 %hand_out.1 = (f32[32,128]{1,0:T(8,128)}, f32[8,4096]{1,0:T(8,128)}, f32[1,8]{1,0:T(1,128)}) custom-call(f32[32,128]{1,0:T(8,128)S(1)} %get-tuple-element.8.amp_v, f32[2,8,16,128]{3,2,1,0:T(8,128)S(1)} %get-tuple-element.9.probs_v), custom_call_target="tpu_custom_call" | custom-call | tf_op jit(solution)/shard_map/hand_out/pallas_call | solution.py:270

commit v3 on v2

--- a/solution.py
+++ b/solution.py
@@ -13,7 +13,7 @@
 PLANE = CHIPS * NC
 G = 128
 PP = G // (NY * NC)
-CHUNKS = 4096 // G // NC
+RUNS = 4096 // G
 MESH = pl.DeviceIdType.MESH
 F32, BF16 = jnp.float32, jnp.bfloat16
 
@@ -26,14 +26,15 @@
     return sorted((o for o in offsets if any(o)), key=hops, reverse=True)
 
 
-OVER_CUTS = far_first([(dz, dx, 0, 0) for dz in range(NZ) for dx in range(NX)])
 IN_PLANE = far_first([(0, dx, dy, dc) for dx in range(NX) for dy in range(NY) for dc in range(NC)])
 SAME_CORE = [o for o in IN_PLANE if o[3] == 0]
 OVER_X = far_first([(0, dx, 0, 0) for dx in range(NX)])
 OVER_Z = far_first([(dz, 0, 0, 0) for dz in range(NZ)])
-GREETED = far_first(set(OVER_CUTS) | set(IN_PLANE))
+NEAR = [o for o in SAME_CORE if hops(o) <= 2]
+DIRECT = [o for o in IN_PLANE if o[:3] not in [n[:3] for n in NEAR]]
+GREETED = far_first(set(OVER_Z) | set(IN_PLANE))
 PARTNER = (0, 0, 0, 1)
-GATE, SEL, SWAP, SUMS, LINES, PROBS, HALF, FIRST = range(8)
+PIECE, GATE, SEL, SWAP, SUMS, CLOSE, LINES, PROBS, FIRST = range(9)
 
 
 def mm(a, b):
@@ -46,13 +47,13 @@
 
 def exchange(
     slot_hbm, state_hbm, gates_hbm, samples_hbm, amp_ref, probs_ref,
-    slot_s, state_v, gate_v, samp_v, asked, part, xr, zs, zr, gr, sel, agg, xs, msg, agx, fin, mags, prow, zbuf,
+    slot_s, state_v, gate_v, samp_v, asked, hot, part, xr, zs, zr, gx, gr, sel, agg, xs, msg, agx, fin, mags, rows, prow,
     load_sem, send_sem, recv_sem,
 ):
     at = [lax.axis_index(name) for name in AXES]
     turn = [[i] + [lax.rem(i + d, n) for d in range(1, n)] for i, n in zip(at, (NZ, NX, NY, NC))]
     z, x, y, core = at
-    zx, chip = z * NX + x, x * NY + y
+    chip = x * NY + y
 
     def peer(offset):
         return tuple(turn[axis][d] for axis, d in enumerate(offset))
@@ -73,8 +74,7 @@
         load_state = pltpu.make_async_copy(state_hbm, state_v, load_sem.at[0])
         load_gate = pltpu.make_async_copy(gates_hbm, gate_v, load_sem.at[1])
         load_slot = pltpu.make_async_copy(slot_hbm, slot_s, load_sem.at[2])
-        half = pl.ds(pl.multiple_of(core * CHUNKS * G, G), CHUNKS * G)
-        load_samp = pltpu.make_async_copy(samples_hbm.at[:, half], samp_v, load_sem.at[3])
+        load_samp = pltpu.make_async_copy(samples_hbm, samp_v, load_sem.at[3])
         for load in (load_state, load_gate, load_slot, load_samp):
             load.start()
         barrier = pltpu.get_barrier_semaphore()
@@ -90,15 +90,21 @@
         pl.semaphore_wait(barrier, len(GREETED))
 
     with scope("send_a"):
-        for offset in OVER_CUTS:
-            _, px, _, _ = peer(offset)
-            send(gate_v.at[core * CHIPS + px * NY + y], gr.at[zx], GATE, offset)
+        for offset in OVER_X:
+            px = peer(offset)[1]
+            send(gate_v.at[core * CHIPS + px * NY + y], gx.at[x], PIECE, offset)
+        keep(gate_v.at[core * CHIPS + chip], gx.at[x], PIECE)
         order = [dz for dz, *_ in OVER_Z] + [0]
         for i, dz in enumerate(order):
             for offset in OVER_X:
                 dx = offset[1]
                 send(part.at[turn[0][dz], turn[1][dx]], xr.at[i, dx - 1], FIRST, offset, FIRST + i)
-        keep(gate_v.at[core * CHIPS + chip], gr.at[zx], GATE)
+    with scope("send_gx"):
+        held = gr.at[pl.ds(z * NX, NX)]
+        wait_bytes(gx, recv_sem.at[PIECE])
+        for offset in OVER_Z:
+            send(gx, held, GATE, offset)
+        keep(gx, held, GATE)
     own = None
     for i, dz in enumerate(order):
         with scope("sums_%d" % i):
@@ -128,13 +134,32 @@
         msg[0:PP] = xs[pl.ds(0, PP, stride=2), :].astype(BF16)
         msg[PP : 2 * PP] = xs[pl.ds(1, PP, stride=2), :].astype(BF16)
         place = chip * NC + core
-        for offset in IN_PLANE:
+        for offset in DIRECT:
             send(msg, agx.at[place], LINES, offset)
+        for offset in NEAR:
+            send(msg, agx.at[place], CLOSE, offset)
         keep(msg, agx.at[place], LINES)
+    with scope("one_hot"):
+        load_samp.wait()
+        for k in range(RUNS):
+            asked[k] = samp_v[:, k * G : (k + 1) * G]
+        places = lax.broadcasted_iota(jnp.int32, (2 * G, G), 0)
+        for k in range(RUNS):
+            wanted = asked[k, pl.ds(z, 1), :]
+            column = (wanted & (G - 1)) + ((wanted >> 15) << 7)
+            hot[:, k * G : (k + 1) * G] = jnp.where(column == places, 1.0, 0.0).astype(BF16)
     with scope("wait_sel"):
         wait_bytes(agg.at[0], recv_sem.at[SEL])
     with scope("swap"):
         send(agg.at[core], agg.at[core], SWAP, PARTNER)
+    with scope("hand_over"):
+        close = agx.at[pl.ds(0, len(NEAR))]
+        wait_bytes(close, recv_sem.at[CLOSE])
+        for offset in NEAR:
+            _, px, py, _ = peer(offset)
+            passed = agx.at[(px * NY + py) * NC + core]
+            send(passed, passed, LINES, PARTNER)
+    with scope("wait_swap"):
         wait_bytes(agg.at[0], recv_sem.at[SWAP])
 
     def gate(g):
@@ -157,10 +182,7 @@
             [jnp.concatenate([prt, -pit], axis=1), jnp.concatenate([pit, prt], axis=1)], axis=0
         ).astype(BF16)
     with scope("wait_lines"):
-        load_samp.wait()
-        for k in range(CHUNKS):
-            asked[k] = samp_v[:, k * G : (k + 1) * G]
-        wait_bytes(agx, recv_sem.at[LINES])
+        wait_bytes(agx.at[pl.ds(0, PLANE - len(NEAR))], recv_sem.at[LINES])
     with scope("math"):
         flat = jnp.concatenate(
             [agx[:, 0:PP].reshape(NX * G, G), agx[:, PP : 2 * PP].reshape(NX * G, G)], axis=1
@@ -176,54 +198,49 @@
             norms = norms + mag
         scale = float(NX * G * G) / jnp.sum(norms, axis=(0, 1), keepdims=True)
     with scope("look_up"):
-        lines = lax.broadcasted_iota(jnp.int32, (8, G), 0)
-        for k in range(CHUNKS):
-            wanted = asked[k, pl.ds(z, 1), :]
-            column = jnp.broadcast_to(wanted & (G - 1), (8, G))
-            line = jnp.broadcast_to(wanted >> 7, (8, G)) - lines
-            picked = jnp.zeros((8, G), F32)
-            for r in range(0, NX * G, 8):
-                found = jnp.take_along_axis(mags[r : r + 8], column, axis=1)
-                picked = jnp.where(line == r, found, picked)
-            prow[k : k + 1] = jnp.sum(picked, axis=0, keepdims=True) * scale
-
-    with scope("send_c"):
-        for offset in OVER_Z:
-            send(prow, zbuf.at[z], PROBS, offset)
-        keep(prow, zbuf.at[z], PROBS)
+        table = (mags[...] * scale).astype(BF16)
+        pairs = jnp.concatenate([table[: 2 * G], table[2 * G :]], axis=1)
+        lines = lax.broadcasted_iota(jnp.int32, (2 * G, G), 0)
+    for part_of, runs in ((0, range(RUNS // 2)), (1, range(RUNS // 2, RUNS))):
+        with scope("look_up_%d" % part_of):
+            for k in runs:
+                found = mm(pairs, hot[:, k * G : (k + 1) * G])
+                line = (asked[k, pl.ds(z, 1), :] >> 7) & (2 * G - 1)
+                rows[k : k + 1] = jnp.sum(jnp.where(line == lines, found, 0.0), axis=0, keepdims=True)
+            some = pl.ds(part_of * RUNS // 2, RUNS // 2)
+            prow[part_of] = rows[some, :].astype(BF16)
+            for offset in OVER_Z:
+                send(prow.at[part_of], probs_ref.at[z, some], PROBS, offset)
+            keep(prow.at[part_of], probs_ref.at[z, some], PROBS)
+    with scope("clear"):
         first = pl.multiple_of((y * NC + core) * PP, PP)
         amp_ref[pl.ds(0, PP, stride=2), :] = fin[x, pl.ds(first, PP), :]
         amp_ref[pl.ds(1, PP, stride=2), :] = fin[x, pl.ds(G + first, PP), :]
-        wait_bytes(gr.at[pl.ds(0, ROWS - 1)], send_sem.at[GATE])
+        wait_bytes(gx.at[pl.ds(0, NX - 1)], send_sem.at[PIECE])
+        wait_bytes(gr.at[pl.ds(0, ROWS - NX)], send_sem.at[GATE])
         wait_bytes(xr, send_sem.at[FIRST])
         wait_bytes(zr, send_sem.at[SUMS])
         wait_bytes(agg.at[0, pl.ds(0, CHIPS - 1)], send_sem.at[SEL])
         wait_bytes(agg.at[0], send_sem.at[SWAP])
-        wait_bytes(agx.at[pl.ds(0, PLANE - 1)], send_sem.at[LINES])
-        wait_bytes(zbuf.at[pl.ds(0, NZ - 1)], send_sem.at[PROBS])
+        wait_bytes(close, send_sem.at[CLOSE])
+        wait_bytes(agx.at[pl.ds(0, len(DIRECT) + len(NEAR))], send_sem.at[LINES])
     with scope("wait_c"):
-        wait_bytes(zbuf, recv_sem.at[PROBS])
-    with scope("send_d"):
-        for c in range(NZ):
-            probs_ref[core, c] = zbuf[c]
-        send(probs_ref.at[core], probs_ref.at[core], HALF, PARTNER)
-    with scope("wait_d"):
-        wait_bytes(probs_ref.at[0], recv_sem.at[HALF])
-        wait_bytes(probs_ref.at[0], send_sem.at[HALF])
-
-
-def hand_out(amp_v, probs_v, amp_hbm, probs_hbm, xeb_ref, lined, sem):
+        wait_bytes(probs_ref, recv_sem.at[PROBS])
+        wait_bytes(probs_ref.at[pl.ds(0, NZ - 1)], send_sem.at[PROBS])
+
+
+def hand_out(amp_v, probs_v, amp_hbm, probs_hbm, xeb_ref, wide, lined, sem):
     keep_amp = pltpu.make_async_copy(amp_v, amp_hbm, sem.at[0])
     keep_amp.start()
+    wide[...] = probs_v[...].astype(F32).reshape(NZ * RUNS, G)
     total = jnp.zeros((NZ, G), F32)
-    for half in range(NC):
-        for k in range(CHUNKS):
-            run = jnp.concatenate([probs_v[half, c, k : k + 1] for c in range(NZ)], axis=0)
-            lined[:, (half * CHUNKS + k) * G : (half * CHUNKS + k + 1) * G] = run
-            total = total + run
+    for k in range(RUNS):
+        run = wide[pl.ds(k, NZ, stride=RUNS), :]
+        lined[:, k * G : (k + 1) * G] = run
+        total = total + run
     keep_probs = pltpu.make_async_copy(lined, probs_hbm, sem.at[1])
     keep_probs.start()
-    means = jnp.sum(total, axis=1, keepdims=True) * (1.0 / (NC * CHUNKS * G))
+    means = jnp.sum(total, axis=1, keepdims=True) * (1.0 / (RUNS * G))
     spot = lax.broadcasted_iota(jnp.int32, (NZ, G), 0) == lax.broadcasted_iota(jnp.int32, (NZ, G), 1)
     xeb_ref[...] = jnp.sum(jnp.where(spot, means, 0.0), axis=0, keepdims=True)[:, :NZ]
     keep_amp.wait()
@@ -237,19 +254,21 @@
     block = (2 * PP, G)
     amp, probs = pl.pallas_call(
         exchange,
-        out_shape=(pltpu.VMEM(block, F32), pltpu.VMEM((NC, NZ, CHUNKS, G), F32)),
+        out_shape=(pltpu.VMEM(block, F32), pltpu.VMEM((NZ, RUNS, G), BF16)),
         in_specs=[hbm] * 4,
         out_specs=(vmem, vmem),
         scratch_shapes=[
             pltpu.SMEM((ROWS,), jnp.int32),
             pltpu.VMEM((NZ, 2, NX) + block, BF16),
             pltpu.VMEM((PLANE, 8, G), BF16),
-            pltpu.VMEM((NZ, CHUNKS * G), jnp.int32),
-            pltpu.VMEM((CHUNKS, NZ, G), jnp.int32),
+            pltpu.VMEM((NZ, RUNS * G), jnp.int32),
+            pltpu.VMEM((RUNS, NZ, G), jnp.int32),
+            pltpu.VMEM((2 * G, RUNS * G), BF16),
             pltpu.VMEM((NZ, NX) + block, BF16),
             pltpu.VMEM((NZ, NX - 1) + block, BF16),
             pltpu.VMEM((NZ - 1,) + block, BF16),
             pltpu.VMEM((NZ - 1,) + block, BF16),
+            pltpu.VMEM((NX, 8, G), BF16),
             pltpu.VMEM((ROWS, 8, G), BF16),
             pltpu.VMEM((4, 8, G), BF16),
             pltpu.VMEM((NC, CHIPS, 4, 8, G), BF16),
@@ -258,8 +277,8 @@
             pltpu.VMEM((PLANE,) + block, BF16),
             pltpu.VMEM((NX, 2 * G, G), F32),
             pltpu.VMEM((NX * G, G), F32),
-            pltpu.VMEM((CHUNKS, G), F32),
-            pltpu.VMEM((NZ, CHUNKS, G), F32),
+            pltpu.VMEM((RUNS, G), F32),
+            pltpu.VMEM((2, RUNS // 2, G), BF16),
             pltpu.SemaphoreType.DMA((4,)),
             pltpu.SemaphoreType.DMA((FIRST + NZ,)),
             pltpu.SemaphoreType.DMA((FIRST + NZ,)),
@@ -271,12 +290,16 @@
         hand_out,
         out_shape=(
             jax.ShapeDtypeStruct(block, F32),
-            jax.ShapeDtypeStruct((NZ, NC * CHUNKS * G), F32),
+            jax.ShapeDtypeStruct((NZ, RUNS * G), F32),
             jax.ShapeDtypeStruct((1, NZ), F32),
         ),
         in_specs=[vmem, vmem],
         out_specs=(hbm, hbm, vmem),
-        scratch_shapes=[pltpu.VMEM((NZ, NC * CHUNKS * G), F32), pltpu.SemaphoreType.DMA((2,))],
+        scratch_shapes=[
+            pltpu.VMEM((NZ * RUNS, G), F32),
+            pltpu.VMEM((NZ, RUNS * G), F32),
+            pltpu.SemaphoreType.DMA((2,)),
+        ],
         name="hand_out",
     )(*(pltpu.with_memory_space_constraint(array, pltpu.VMEM) for array in (amp, probs)))
     return amp.reshape(1, PP, 2, G), probs, xeb.reshape(NZ)

time: 36.4 us -> 33.7 us (0.926)
  Pallas kernels: 35.6 us -> 32.9 us
    pallas_call x1, Pallas kernels: 34.4 us -> 31.7 us  [on_device(): pl.pallas_call(exchange, out_shape=(pltpu.VMEM(block, F32), pltpu.VMEM((N...]
where the time goes in v3:
time: 33.7 us; the launch traced here: 33.6 us
  Pallas kernels  32.9 us (98%)
  between operations  0.64 us (2%)
    pallas_call x1, Pallas kernels, on_device(): pl.pallas_call(exchange, out_shape=(pltpu.VMEM(block, F32), pltpu.VMEM((N...  31.7 us
    pallas_call x1, Pallas kernels, on_device(): pl.pallas_call(hand_out, out_shape=(jax.ShapeDtypeStruct(block, F32), jax...  1.28 us

profile of v3, /device:TPU:1, one launch (start us, length us, event | category | flops | bytes accessed | tf_op | source)
XLA Modules:
  0.0 33.6 jit_solution(123656807927110225)
XLA Ops:
  0.6 31.7 %amplitudes.1 = (f32[32,128]{1,0:T(8,128)S(1)}, bf16[8,32,128]{2,1,0:T(8,128)(2,1)S(1)}) custom-call(s32[32]{0:T(128)} %slot_hbm.1, bf16[8,2,4,32,128]{4,3,2,1,0:T(8,128)(2,1)} %bitcast.4, bf16[32,8,128]{2,1,0:T(8,128)(2,1)} %bitcast.5, s32[8,4096]{1,0:T(8,128)} %samples_hbm.1), custom_call_target="tpu_custom_call" | custom-call | tf_op jit(solution)/shard_map/amplitudes/pallas_call | solution.py:255
  32.3 1.3 %hand_out.1 = (f32[32,128]{1,0:T(8,128)}, f32[8,4096]{1,0:T(8,128)}, f32[1,8]{1,0:T(1,128)}) custom-call(f32[32,128]{1,0:T(8,128)S(1)} %get-tuple-element.8.amp_v, bf16[8,32,128]{2,1,0:T(8,128)(2,1)S(1)} %get-tuple-element.9.probs_v), custom_call_target="tpu_custom_call" | custom-call | tf_op jit(solution)/shard_map/hand_out/pallas_call | solution.py:289
